TPU v7x, 8 devices: a whole 2x2x1 slice. The times are simulated.
8 devices in a mesh: hp: 1 (over z), cp: 8 (over y, x, core).
Axes of the slice: x: 2, y: 2, z: 1, core: 2. Of those that a mesh axis runs over, the one named last changes fastest.
Arguments:
- q: bfloat16 [6144, 8, 128], P('cp', 'hp')
- k: bfloat16 [6144, 8, 128], P('cp', 'hp')
- v: bfloat16 [6144, 8, 128], P('cp', 'hp')
- u_bias: float32 [8, 128], P('hp')
- v_bias: float32 [8, 128], P('hp')
- rel_table: bfloat16 [6144, 1024], P('cp')
- w_rel: bfloat16 [1024, 8, 128], P(None, 'hp')
- d_out: bfloat16 [6144, 8, 128], P('cp', 'hp')
Outputs:
- output 1: bfloat16 [6144, 8, 128], P('cp', 'hp')
- output 2: bfloat16 [6144, 8, 128], P('cp', 'hp')
- output 3: bfloat16 [6144, 8, 128], P('cp', 'hp')
- output 4: bfloat16 [6144, 8, 128], P('cp', 'hp')
- output 5: float32 [8, 128], P('hp')
- output 6: float32 [8, 128], P('hp')
- output 7: float32 [1024, 8, 128], P(None, 'hp')
All inputs are finite; a program needn't handle non-finite values.
Results may differ from a plain program's by a relative error of at most 0.0149584.
Values are sent between devices in bfloat16 or wider.
A program may use at most 1 GiB of HBM per device.

v0:
```python
import jax
import jax.numpy as jnp
from jax import lax
from jax.sharding import PartitionSpec as P


def skew_scores(by_offset):
    lead_dims = by_offset.shape[:-2]
    block_len = by_offset.shape[-2]
    flat_view = by_offset.reshape(lead_dims + (2 * block_len * block_len,))
    kept_view = flat_view[..., block_len - 1:block_len - 1 + block_len * (2 * block_len - 1)]
    return kept_view.reshape(lead_dims + (block_len, 2 * block_len - 1))[..., :block_len]


def unskew_scores(by_key):
    lead_dims = by_key.shape[:-2]
    block_len = by_key.shape[-1]
    pad_lead = [(0, 0)] * len(lead_dims)
    widened = jnp.pad(by_key, pad_lead + [(0, 0), (0, block_len - 1)])
    flat_view = widened.reshape(lead_dims + (block_len * (2 * block_len - 1),))
    flat_view = jnp.pad(flat_view, pad_lead + [(block_len - 1, 1)])
    return flat_view.reshape(lead_dims + (block_len, 2 * block_len))


def solution(mesh):
    n_dev = mesh.shape['cp']
    shift_pairs = [(src_dev, (src_dev + 1) % n_dev) for src_dev in range(n_dev)]
    last_step = n_dev - 1
    seq_spec = P('cp', 'hp', None)
    head_spec = P('hp', None)
    weight_spec = P(None, 'hp', None)

    def local_fn(q, k, v, u_bias, v_bias, rel_table, w_rel, d_out):
        block_len, num_heads, head_dim = q.shape
        inv_sqrt = head_dim ** -0.5
        my_block = lax.axis_index('cp')
        rel_mine = jnp.einsum('uo,ojf->ujf', rel_table, w_rel, preferred_element_type=jnp.float32).astype(jnp.bfloat16)
        rel_flipped = lax.all_gather(rel_mine[::-1], 'cp')
        q_wide = q.astype(jnp.float32)
        q_u = (q_wide + u_bias).astype(jnp.bfloat16)
        q_v = (q_wide + v_bias).astype(jnp.bfloat16)
        row_ids = jnp.arange(block_len)
        above_diag = row_ids[None, :] > row_ids[:, None]

        def rel_window(distance):
            near_blk = lax.dynamic_index_in_dim(rel_flipped, distance, 0, keepdims=False)
            far_blk = lax.dynamic_index_in_dim(rel_flipped, jnp.maximum(distance - 1, 0), 0, keepdims=False)
            return jnp.concatenate([near_blk, far_blk], axis=0)

        def block_scores(k_blk, window, distance):
            content = jnp.einsum('qhd,khd->hqk', q_u, k_blk, preferred_element_type=jnp.float32)
            by_offset = jnp.einsum('qhd,shd->hqs', q_v, window, preferred_element_type=jnp.float32)
            score_ij = (content + skew_scores(by_offset)) * inv_sqrt
            return jnp.where(above_diag & (distance == 0), -jnp.inf, score_ij)

        def attend(distance, k_blk, v_blk, run_stats):
            run_max, run_sum, out_acc = run_stats
            score_ij = block_scores(k_blk, rel_window(distance), distance)
            new_max = jnp.maximum(run_max, score_ij.max(axis=-1))
            prob_ij = jnp.exp(score_ij - new_max[..., None])
            rescale = jnp.exp(run_max - new_max)
            run_sum = rescale * run_sum + prob_ij.sum(axis=-1)
            out_acc = out_acc * rescale.T[:, :, None] + jnp.einsum('hqk,khd->qhd', prob_ij.astype(jnp.bfloat16), v_blk, preferred_element_type=jnp.float32)
            return new_max, run_sum, out_acc

        def fwd_step(step_idx, carry):
            k_blk, v_blk, run_stats = carry
            run_stats = lax.cond(step_idx <= my_block, lambda stats_in: attend(step_idx, k_blk, v_blk, stats_in), lambda stats_in: stats_in, run_stats)
            k_blk = lax.ppermute(k_blk, 'cp', shift_pairs)
            v_blk = lax.ppermute(v_blk, 'cp', shift_pairs)
            return k_blk, v_blk, run_stats

        run_stats = (
            jnp.full((num_heads, block_len), -jnp.inf, jnp.float32),
            jnp.zeros((num_heads, block_len), jnp.float32),
            jnp.zeros((block_len, num_heads, head_dim), jnp.float32),
        )
        k_blk, v_blk, run_stats = lax.fori_loop(0, last_step, fwd_step, (k, v, run_stats))
        run_stats = lax.cond(last_step <= my_block, lambda stats_in: attend(last_step, k_blk, v_blk, stats_in), lambda stats_in: stats_in, run_stats)
        run_max, run_sum, out_acc = run_stats
        out_full = out_acc / run_sum.T[:, :, None]
        log_norm = run_max + jnp.log(run_sum)
        row_delta = jnp.sum(d_out.astype(jnp.float32) * out_full, axis=-1).T

        def grad_block(distance, k_blk, v_blk, grad_state):
            dk_acc, dv_acc, grad_qu, grad_qv, grad_rel = grad_state
            window = rel_window(distance)
            score_ij = block_scores(k_blk, window, distance)
            prob_ij = jnp.exp(score_ij - log_norm[..., None])
            d_prob = jnp.einsum('qhd,khd->hqk', d_out, v_blk, preferred_element_type=jnp.float32)
            d_score = (prob_ij * (d_prob - row_delta[..., None]) * inv_sqrt).astype(jnp.bfloat16)
            dv_acc = dv_acc + jnp.einsum('hqk,qhd->khd', prob_ij.astype(jnp.bfloat16), d_out, preferred_element_type=jnp.float32)
            dk_acc = dk_acc + jnp.einsum('hqk,qhd->khd', d_score, q_u, preferred_element_type=jnp.float32)
            grad_qu = grad_qu + jnp.einsum('hqk,khd->qhd', d_score, k_blk, preferred_element_type=jnp.float32)
            d_wide = unskew_scores(d_score)
            grad_qv = grad_qv + jnp.einsum('hqs,shd->qhd', d_wide, window, preferred_element_type=jnp.float32)
            d_window = jnp.einsum('hqs,qhd->shd', d_wide, q_v, preferred_element_type=jnp.float32)
            near_sum = lax.dynamic_index_in_dim(grad_rel, distance, 0, keepdims=False) + d_window[:block_len]
            grad_rel = lax.dynamic_update_index_in_dim(grad_rel, near_sum, distance, 0)
            far_idx = jnp.maximum(distance - 1, 0)
            far_sum = lax.dynamic_index_in_dim(grad_rel, far_idx, 0, keepdims=False) + d_window[block_len:]
            grad_rel = lax.dynamic_update_index_in_dim(grad_rel, far_sum, far_idx, 0)
            return dk_acc, dv_acc, grad_qu, grad_qv, grad_rel

        def bwd_step(step_idx, carry):
            k_blk, v_blk, grad_state = carry
            grad_state = lax.cond(step_idx <= my_block, lambda grads_in: grad_block(step_idx, k_blk, v_blk, grads_in), lambda grads_in: grads_in, grad_state)
            dk_acc, dv_acc, grad_qu, grad_qv, grad_rel = grad_state
            k_blk = lax.ppermute(k_blk, 'cp', shift_pairs)
            v_blk = lax.ppermute(v_blk, 'cp', shift_pairs)
            dk_acc = lax.ppermute(dk_acc, 'cp', shift_pairs)
            dv_acc = lax.ppermute(dv_acc, 'cp', shift_pairs)
            return k_blk, v_blk, (dk_acc, dv_acc, grad_qu, grad_qv, grad_rel)

        blk_zeros = jnp.zeros((block_len, num_heads, head_dim), jnp.float32)
        grad_state = (blk_zeros, blk_zeros, blk_zeros, blk_zeros, jnp.zeros((n_dev, block_len, num_heads, head_dim), jnp.float32))
        k_blk, v_blk, grad_state = lax.fori_loop(0, last_step, bwd_step, (k, v, grad_state))
        grad_state = lax.cond(last_step <= my_block, lambda grads_in: grad_block(last_step, k_blk, v_blk, grads_in), lambda grads_in: grads_in, grad_state)
        dk_acc, dv_acc, grad_qu, grad_qv, grad_rel = grad_state
        dk_acc = lax.ppermute(dk_acc, 'cp', shift_pairs)
        dv_acc = lax.ppermute(dv_acc, 'cp', shift_pairs)
        rel_grad_mine = lax.psum_scatter(grad_rel, 'cp', scatter_dimension=0, tiled=False)
        d_rel = rel_grad_mine[::-1].astype(jnp.bfloat16)
        d_w_rel = lax.psum(jnp.einsum('uo,ujf->ojf', rel_table, d_rel, preferred_element_type=jnp.float32), 'cp')
        d_u_bias = lax.psum(grad_qu.sum(axis=0), 'cp')
        d_v_bias = lax.psum(grad_qv.sum(axis=0), 'cp')
        return (
            out_full.astype(jnp.bfloat16),
            (grad_qu + grad_qv).astype(jnp.bfloat16),
            dk_acc.astype(jnp.bfloat16),
            dv_acc.astype(jnp.bfloat16),
            d_u_bias,
            d_v_bias,
            d_w_rel,
        )

    return jax.shard_map(
        local_fn,
        mesh=mesh,
        in_specs=(seq_spec, seq_spec, seq_spec, head_spec, head_spec, P('cp', None), weight_spec, seq_spec),
        out_specs=(seq_spec, seq_spec, seq_spec, seq_spec, head_spec, head_spec, weight_spec),
        check_vma=False,
    )
```

profile of v0, /device:TPU:0, one launch (start us, length us, event | category | flops | bytes accessed | tf_op | source)
XLA Modules:
  0.0 7099.0 jit_solution(9227835148760462164)
XLA Ops:
  120.3 1930.3 %while.48 = (s32[]{:T(128)}, bf16[768,8,128]{2,0,1:T(8,128)(2,1)}, bf16[768,8,128]{2,0,1:T(8,128)(2,1)}, f32[8,768]{1,0:T(8,128)}, f32[8,768]{1,0:T(8,128)}, /*i...) while((s32[]{:T(128)}, bf16[768,8,128]{2,0,1:T(8,128)(2,1)}, ...), condition=%wide.region_5.6_spmd.clone, body=%wide.region_0.5_spmd.clone.sunk | while | flops 4878649344 | bytes 649740736 | solution.py:78
  130.7 297.0 %conditional.10 = ((f32[8,768]{1,0:T(8,128)}, f32[8,768]{1,0:T(8,128)}, f32[768,8,128]{2,0,1:T(8,128)})) conditional(s32[]{:T(128)} %convert_element_type.120, (f32[8,768]{1,0:T(8,128)}, f32[8,768]{1,0:T(8,128)}, f32[768,8,128]{2,0,1:T(8,128)}) %tuple.144, (s32[]{:T(128)}, s32[768,768]{0,1:T(8,128)}, bf16[768,8,128]{2,0,1:T(8,128)(2,1)S(1)}, ...), branch_computations={%region_1.0_spmd, %region_2.4_spmd} | conditional | flops 4878649344 | bytes 619856000 | solution.py:68
  239.2 62.0 reshape.65
  478.7 274.2 %collective-permute-start = (bf16[768,8,128]{2,0,1:T(8,128)(2,1)}, bf16[768,8,128]{2,0,1:T(8,128)(2,1)}, u32[]{:S(2)}, u32[]{:S(2)}) collective-permute-start(bf16[768,8,128]{2,0,1:T(8,128)(2,1)} %copy.217), channel_id=1, source_target_pairs={{0,1},{1,2},{2,3},{3,4},{4,5},{5,6},{6,7},{7,0}} | collective-permute-start | bytes 4718600 | tf_op jit(solution)/shard_map/while/body/eval_jaxpr/ppermute | solution.py:69
  794.8 276.9 %collective-permute-start.1 = (bf16[768,8,128]{2,0,1:T(8,128)(2,1)}, bf16[768,8,128]{2,0,1:T(8,128)(2,1)}, u32[]{:S(2)}, u32[]{:S(2)}) collective-permute-start(bf16[768,8,128]{2,0,1:T(8,128)(2,1)} %copy.218), channel_id=1, source_target_pairs={{0,1},{1,2},{2,3},{3,4},{4,5},{5,6},{6,7},{7,0}} | collective-permute-start | bytes 4718600 | tf_op jit(solution)/shard_map/while/body/eval_jaxpr/ppermute | solution.py:70
  1114.5 286.0 %collective-permute-done = bf16[768,8,128]{2,0,1:T(8,128)(2,1)} collective-permute-done((bf16[768,8,128]{2,0,1:T(8,128)(2,1)}, bf16[768,8,128]{2,0,1:T(8,128)(2,1)}, u32[]{:S(2)}, u32[]{:S(2)}) %collective-permute-start) | collective-permute-done | bytes 1572896 | tf_op jit(solution)/shard_map/while/body/eval_jaxpr/ppermute | solution.py:69
  1426.0 288.1 %collective-permute-done = bf16[768,8,128]{2,0,1:T(8,128)(2,1)} collective-permute-done((bf16[768,8,128]{2,0,1:T(8,128)(2,1)}, bf16[768,8,128]{2,0,1:T(8,128)(2,1)}, u32[]{:S(2)}, u32[]{:S(2)}) %collective-permute-start) | collective-permute-done | bytes 1572896 | tf_op jit(solution)/shard_map/while/body/eval_jaxpr/ppermute | solution.py:69
  1739.6 287.8 %collective-permute-done = bf16[768,8,128]{2,0,1:T(8,128)(2,1)} collective-permute-done((bf16[768,8,128]{2,0,1:T(8,128)(2,1)}, bf16[768,8,128]{2,0,1:T(8,128)(2,1)}, u32[]{:S(2)}, u32[]{:S(2)}) %collective-permute-start) | collective-permute-done | bytes 1572896 | tf_op jit(solution)/shard_map/while/body/eval_jaxpr/ppermute | solution.py:69
  2091.5 4304.0 %while.49 = (s32[]{:T(128)}, bf16[768,8,128]{2,0,1:T(8,128)(2,1)}, bf16[768,8,128]{2,0,1:T(8,128)(2,1)}, f32[768,8,128]{2,0,1:T(8,128)}, f32[768,8,128]{2,0,1:T(...) while((s32[]{:T(128)}, bf16[768,8,128]{2,0,1:T(8,128)(2,1)}, ...), condition=%wide.region_14.15_spmd.clone, body=%wide.region_11.14_spmd.clone.sunk | while | flops 13348503552 | bytes 893018624 | solution.py:117
  2100.4 424.4 %conditional.11 = ((f32[768,8,128]{2,0,1:T(8,128)}, f32[768,8,128]{2,0,1:T(8,128)}, f32[768,8,128]{2,0,1:T(8,128)}, f32[768,8,128]{0,2,1:T(8,128)}, f32[8,768,8,128]{3,1,2,0:T(8,128)})) conditional(s32[]{:T(128)} %convert_element_type.121, (f32[768,8,128]{2,0,1:T(8,128)}, f32[768,8,128]{2,0,1:T(8,128)}, f32[768,8,128]{2,0,1:T(8,128)}, ...), branch_computations={%region_12.12_spmd, %region_13.13_spmd} | conditional | flops 13348503552 | bytes 825188480 | solution.py:107
  2208.7 62.0 reshape.67
  2524.9 586.2 %collective-permute-done.4 = f32[768,8,128]{2,0,1:T(8,128)S(1)} collective-permute-done((f32[768,8,128]{2,0,1:T(8,128)}, f32[768,8,128]{2,0,1:T(8,128)S(1)}, u32[]{:S(2)}, u32[]{:S(2)}) %collective-permute-start.4) | collective-permute-done | bytes 3145760 | tf_op jit(solution)/shard_map/while/body/eval_jaxpr/ppermute | solution.py:111
  3242.2 287.4 %collective-permute-start.2 = (bf16[768,8,128]{2,0,1:T(8,128)(2,1)}, bf16[768,8,128]{2,0,1:T(8,128)(2,1)}, u32[]{:S(2)}, u32[]{:S(2)}) collective-permute-start(bf16[768,8,128]{2,0,1:T(8,128)(2,1)} %copy.243), channel_id=1, source_target_pairs={{0,1},{1,2},{2,3},{3,4},{4,5},{5,6},{6,7},{7,0}} | collective-permute-start | bytes 4718600 | tf_op jit(solution)/shard_map/while/body/eval_jaxpr/ppermute | solution.py:109
  3533.2 112.9 %collective-permute-done.4 = f32[768,8,128]{2,0,1:T(8,128)S(1)} collective-permute-done((f32[768,8,128]{2,0,1:T(8,128)}, f32[768,8,128]{2,0,1:T(8,128)S(1)}, u32[]{:S(2)}, u32[]{:S(2)}) %collective-permute-start.4) | collective-permute-done | bytes 3145760 | tf_op jit(solution)/shard_map/while/body/eval_jaxpr/ppermute | solution.py:111
  3722.0 311.2 %collective-permute-start.5 = (f32[768,8,128]{2,0,1:T(8,128)}, f32[768,8,128]{2,0,1:T(8,128)}, u32[]{:S(2)}, u32[]{:S(2)}) collective-permute-start(f32[768,8,128]{2,0,1:T(8,128)} %get-tuple-element.1177), channel_id=1, source_target_pairs={{0,1},{1,2},{2,3},{3,4},{4,5},{5,6},{6,7},{7,0}} | collective-permute-start | bytes 9437192 | tf_op jit(solution)/shard_map/while/body/eval_jaxpr/ppermute | solution.py:112
  4084.4 96.8 %collective-permute-done.4 = f32[768,8,128]{2,0,1:T(8,128)S(1)} collective-permute-done((f32[768,8,128]{2,0,1:T(8,128)}, f32[768,8,128]{2,0,1:T(8,128)S(1)}, u32[]{:S(2)}, u32[]{:S(2)}) %collective-permute-start.4) | collective-permute-done | bytes 3145760 | tf_op jit(solution)/shard_map/while/body/eval_jaxpr/ppermute | solution.py:111
  4257.2 362.0 %collective-permute-start.2 = (bf16[768,8,128]{2,0,1:T(8,128)(2,1)}, bf16[768,8,128]{2,0,1:T(8,128)(2,1)}, u32[]{:S(2)}, u32[]{:S(2)}) collective-permute-start(bf16[768,8,128]{2,0,1:T(8,128)(2,1)} %copy.243), channel_id=1, source_target_pairs={{0,1},{1,2},{2,3},{3,4},{4,5},{5,6},{6,7},{7,0}} | collective-permute-start | bytes 4718600 | tf_op jit(solution)/shard_map/while/body/eval_jaxpr/ppermute | solution.py:109
  4622.8 93.2 %collective-permute-done.4 = f32[768,8,128]{2,0,1:T(8,128)S(1)} collective-permute-done((f32[768,8,128]{2,0,1:T(8,128)}, f32[768,8,128]{2,0,1:T(8,128)S(1)}, u32[]{:S(2)}, u32[]{:S(2)}) %collective-permute-start.4) | collective-permute-done | bytes 3145760 | tf_op jit(solution)/shard_map/while/body/eval_jaxpr/ppermute | solution.py:111
  4791.9 369.3 %collective-permute-start.3 = (bf16[768,8,128]{2,0,1:T(8,128)(2,1)}, bf16[768,8,128]{2,0,1:T(8,128)(2,1)}, u32[]{:S(2)}, u32[]{:S(2)}) collective-permute-start(bf16[768,8,128]{2,0,1:T(8,128)(2,1)} %copy.244), channel_id=1, source_target_pairs={{0,1},{1,2},{2,3},{3,4},{4,5},{5,6},{6,7},{7,0}} | collective-permute-start | bytes 4718600 | tf_op jit(solution)/shard_map/while/body/eval_jaxpr/ppermute | solution.py:110
  5161.2 89.7 %collective-permute-done.4 = f32[768,8,128]{2,0,1:T(8,128)S(1)} collective-permute-done((f32[768,8,128]{2,0,1:T(8,128)}, f32[768,8,128]{2,0,1:T(8,128)S(1)}, u32[]{:S(2)}, u32[]{:S(2)}) %collective-permute-start.4) | collective-permute-done | bytes 3145760 | tf_op jit(solution)/shard_map/while/body/eval_jaxpr/ppermute | solution.py:111
  5326.9 459.0 %collective-permute-done.4 = f32[768,8,128]{2,0,1:T(8,128)S(1)} collective-permute-done((f32[768,8,128]{2,0,1:T(8,128)}, f32[768,8,128]{2,0,1:T(8,128)S(1)}, u32[]{:S(2)}, u32[]{:S(2)}) %collective-permute-start.4) | collective-permute-done | bytes 3145760 | tf_op jit(solution)/shard_map/while/body/eval_jaxpr/ppermute | solution.py:111
  5861.9 458.8 %collective-permute-done.4 = f32[768,8,128]{2,0,1:T(8,128)S(1)} collective-permute-done((f32[768,8,128]{2,0,1:T(8,128)}, f32[768,8,128]{2,0,1:T(8,128)S(1)}, u32[]{:S(2)}, u32[]{:S(2)}) %collective-permute-start.4) | collective-permute-done | bytes 3145760 | tf_op jit(solution)/shard_map/while/body/eval_jaxpr/ppermute | solution.py:111
  6411.1 556.5 %reduce-scatter.2.cloned.1.call-done = f32[1,768,8,128]{3,1,2,0:T(8,128)} async-done(((f32[8,768,8,128]{3,1,2,0:T(8,128)}), f32[1,768,8,128]{3,1,2,0:T(8,128)}) %reduce-scatter.2.cloned.1.call-update) | async-done | bytes 3145744 | tf_op jit(solution)/shard_map/reduce_scatter | solution.py:122
  7006.2 70.3 all-reduce.4
  (337 shorter events, 1672.4 us)
Async XLA Ops:
  36.3 6931.2 %reduce-scatter.2.cloned.1.call-start = ((), (), s32[]{:S(2)}) async-start(), calls=%async_computation.1 | async-start | bytes 28311552 | tf_op jit(solution)/shard_map/reduce_scatter | solution.py:122
  2524.7 586.4 %collective-permute-start.4 = (f32[768,8,128]{2,0,1:T(8,128)}, f32[768,8,128]{2,0,1:T(8,128)S(1)}, u32[]{:S(2)}, u32[]{:S(2)}) collective-permute-start(f32[768,8,128]{2,0,1:T(8,128)} %get-tuple-element.1176), channel_id=1, source_target_pairs={{0,1},{1,2},{2,3},{3,4},{4,5},{5,6},{6,7},{7,0}} | collective-permute-start | bytes 9437192 | tf_op jit(solution)/shard_map/while/body/eval_jaxpr/ppermute | solution.py:111
  2524.8 620.1 %collective-permute-start.5 = (f32[768,8,128]{2,0,1:T(8,128)}, f32[768,8,128]{2,0,1:T(8,128)}, u32[]{:S(2)}, u32[]{:S(2)}) collective-permute-start(f32[768,8,128]{2,0,1:T(8,128)} %get-tuple-element.1177), channel_id=1, source_target_pairs={{0,1},{1,2},{2,3},{3,4},{4,5},{5,6},{6,7},{7,0}} | collective-permute-start | bytes 9437192 | tf_op jit(solution)/shard_map/while/body/eval_jaxpr/ppermute | solution.py:112
  2524.8 636.9 %collective-permute-start.2 = (bf16[768,8,128]{2,0,1:T(8,128)(2,1)}, bf16[768,8,128]{2,0,1:T(8,128)(2,1)}, u32[]{:S(2)}, u32[]{:S(2)}) collective-permute-start(bf16[768,8,128]{2,0,1:T(8,128)(2,1)} %copy.243), channel_id=1, source_target_pairs={{0,1},{1,2},{2,3},{3,4},{4,5},{5,6},{6,7},{7,0}} | collective-permute-start | bytes 4718600 | tf_op jit(solution)/shard_map/while/body/eval_jaxpr/ppermute | solution.py:109
  2524.8 653.7 %collective-permute-start.3 = (bf16[768,8,128]{2,0,1:T(8,128)(2,1)}, bf16[768,8,128]{2,0,1:T(8,128)(2,1)}, u32[]{:S(2)}, u32[]{:S(2)}) collective-permute-start(bf16[768,8,128]{2,0,1:T(8,128)(2,1)} %copy.244), channel_id=1, source_target_pairs={{0,1},{1,2},{2,3},{3,4},{4,5},{5,6},{6,7},{7,0}} | collective-permute-start | bytes 4718600 | tf_op jit(solution)/shard_map/while/body/eval_jaxpr/ppermute | solution.py:110
  3187.5 492.3 %collective-permute-start.5 = (f32[768,8,128]{2,0,1:T(8,128)}, f32[768,8,128]{2,0,1:T(8,128)}, u32[]{:S(2)}, u32[]{:S(2)}) collective-permute-start(f32[768,8,128]{2,0,1:T(8,128)} %get-tuple-element.1177), channel_id=1, source_target_pairs={{0,1},{1,2},{2,3},{3,4},{4,5},{5,6},{6,7},{7,0}} | collective-permute-start | bytes 9437192 | tf_op jit(solution)/shard_map/while/body/eval_jaxpr/ppermute | solution.py:112
  3722.0 459.2 %collective-permute-start.4 = (f32[768,8,128]{2,0,1:T(8,128)}, f32[768,8,128]{2,0,1:T(8,128)S(1)}, u32[]{:S(2)}, u32[]{:S(2)}) collective-permute-start(f32[768,8,128]{2,0,1:T(8,128)} %get-tuple-element.1176), channel_id=1, source_target_pairs={{0,1},{1,2},{2,3},{3,4},{4,5},{5,6},{6,7},{7,0}} | collective-permute-start | bytes 9437192 | tf_op jit(solution)/shard_map/while/body/eval_jaxpr/ppermute | solution.py:111
  3722.0 492.9 %collective-permute-start.5 = (f32[768,8,128]{2,0,1:T(8,128)}, f32[768,8,128]{2,0,1:T(8,128)}, u32[]{:S(2)}, u32[]{:S(2)}) collective-permute-start(f32[768,8,128]{2,0,1:T(8,128)} %get-tuple-element.1177), channel_id=1, source_target_pairs={{0,1},{1,2},{2,3},{3,4},{4,5},{5,6},{6,7},{7,0}} | collective-permute-start | bytes 9437192 | tf_op jit(solution)/shard_map/while/body/eval_jaxpr/ppermute | solution.py:112
  4257.2 458.8 %collective-permute-start.4 = (f32[768,8,128]{2,0,1:T(8,128)}, f32[768,8,128]{2,0,1:T(8,128)S(1)}, u32[]{:S(2)}, u32[]{:S(2)}) collective-permute-start(f32[768,8,128]{2,0,1:T(8,128)} %get-tuple-element.1176), channel_id=1, source_target_pairs={{0,1},{1,2},{2,3},{3,4},{4,5},{5,6},{6,7},{7,0}} | collective-permute-start | bytes 9437192 | tf_op jit(solution)/shard_map/while/body/eval_jaxpr/ppermute | solution.py:111
  4257.2 492.5 %collective-permute-start.5 = (f32[768,8,128]{2,0,1:T(8,128)}, f32[768,8,128]{2,0,1:T(8,128)}, u32[]{:S(2)}, u32[]{:S(2)}) collective-permute-start(f32[768,8,128]{2,0,1:T(8,128)} %get-tuple-element.1177), channel_id=1, source_target_pairs={{0,1},{1,2},{2,3},{3,4},{4,5},{5,6},{6,7},{7,0}} | collective-permute-start | bytes 9437192 | tf_op jit(solution)/shard_map/while/body/eval_jaxpr/ppermute | solution.py:112
  4257.2 509.4 %collective-permute-start.2 = (bf16[768,8,128]{2,0,1:T(8,128)(2,1)}, bf16[768,8,128]{2,0,1:T(8,128)(2,1)}, u32[]{:S(2)}, u32[]{:S(2)}) collective-permute-start(bf16[768,8,128]{2,0,1:T(8,128)(2,1)} %copy.243), channel_id=1, source_target_pairs={{0,1},{1,2},{2,3},{3,4},{4,5},{5,6},{6,7},{7,0}} | collective-permute-start | bytes 4718600 | tf_op jit(solution)/shard_map/while/body/eval_jaxpr/ppermute | solution.py:109
  4791.9 459.0 %collective-permute-start.4 = (f32[768,8,128]{2,0,1:T(8,128)}, f32[768,8,128]{2,0,1:T(8,128)S(1)}, u32[]{:S(2)}, u32[]{:S(2)}) collective-permute-start(f32[768,8,128]{2,0,1:T(8,128)} %get-tuple-element.1176), channel_id=1, source_target_pairs={{0,1},{1,2},{2,3},{3,4},{4,5},{5,6},{6,7},{7,0}} | collective-permute-start | bytes 9437192 | tf_op jit(solution)/shard_map/while/body/eval_jaxpr/ppermute | solution.py:111
  4791.9 492.7 %collective-permute-start.5 = (f32[768,8,128]{2,0,1:T(8,128)}, f32[768,8,128]{2,0,1:T(8,128)}, u32[]{:S(2)}, u32[]{:S(2)}) collective-permute-start(f32[768,8,128]{2,0,1:T(8,128)} %get-tuple-element.1177), channel_id=1, source_target_pairs={{0,1},{1,2},{2,3},{3,4},{4,5},{5,6},{6,7},{7,0}} | collective-permute-start | bytes 9437192 | tf_op jit(solution)/shard_map/while/body/eval_jaxpr/ppermute | solution.py:112
  4791.9 509.5 %collective-permute-start.2 = (bf16[768,8,128]{2,0,1:T(8,128)(2,1)}, bf16[768,8,128]{2,0,1:T(8,128)(2,1)}, u32[]{:S(2)}, u32[]{:S(2)}) collective-permute-start(bf16[768,8,128]{2,0,1:T(8,128)(2,1)} %copy.243), channel_id=1, source_target_pairs={{0,1},{1,2},{2,3},{3,4},{4,5},{5,6},{6,7},{7,0}} | collective-permute-start | bytes 4718600 | tf_op jit(solution)/shard_map/while/body/eval_jaxpr/ppermute | solution.py:109
  4791.9 526.4 %collective-permute-start.3 = (bf16[768,8,128]{2,0,1:T(8,128)(2,1)}, bf16[768,8,128]{2,0,1:T(8,128)(2,1)}, u32[]{:S(2)}, u32[]{:S(2)}) collective-permute-start(bf16[768,8,128]{2,0,1:T(8,128)(2,1)} %copy.244), channel_id=1, source_target_pairs={{0,1},{1,2},{2,3},{3,4},{4,5},{5,6},{6,7},{7,0}} | collective-permute-start | bytes 4718600 | tf_op jit(solution)/shard_map/while/body/eval_jaxpr/ppermute | solution.py:110
  5326.8 459.1 %collective-permute-start.4 = (f32[768,8,128]{2,0,1:T(8,128)}, f32[768,8,128]{2,0,1:T(8,128)S(1)}, u32[]{:S(2)}, u32[]{:S(2)}) collective-permute-start(f32[768,8,128]{2,0,1:T(8,128)} %get-tuple-element.1176), channel_id=1, source_target_pairs={{0,1},{1,2},{2,3},{3,4},{4,5},{5,6},{6,7},{7,0}} | collective-permute-start | bytes 9437192 | tf_op jit(solution)/shard_map/while/body/eval_jaxpr/ppermute | solution.py:111
  5326.8 492.8 %collective-permute-start.5 = (f32[768,8,128]{2,0,1:T(8,128)}, f32[768,8,128]{2,0,1:T(8,128)}, u32[]{:S(2)}, u32[]{:S(2)}) collective-permute-start(f32[768,8,128]{2,0,1:T(8,128)} %get-tuple-element.1177), channel_id=1, source_target_pairs={{0,1},{1,2},{2,3},{3,4},{4,5},{5,6},{6,7},{7,0}} | collective-permute-start | bytes 9437192 | tf_op jit(solution)/shard_map/while/body/eval_jaxpr/ppermute | solution.py:112
  5326.8 509.6 %collective-permute-start.2 = (bf16[768,8,128]{2,0,1:T(8,128)(2,1)}, bf16[768,8,128]{2,0,1:T(8,128)(2,1)}, u32[]{:S(2)}, u32[]{:S(2)}) collective-permute-start(bf16[768,8,128]{2,0,1:T(8,128)(2,1)} %copy.243), channel_id=1, source_target_pairs={{0,1},{1,2},{2,3},{3,4},{4,5},{5,6},{6,7},{7,0}} | collective-permute-start | bytes 4718600 | tf_op jit(solution)/shard_map/while/body/eval_jaxpr/ppermute | solution.py:109
  5326.9 526.5 %collective-permute-start.3 = (bf16[768,8,128]{2,0,1:T(8,128)(2,1)}, bf16[768,8,128]{2,0,1:T(8,128)(2,1)}, u32[]{:S(2)}, u32[]{:S(2)}) collective-permute-start(bf16[768,8,128]{2,0,1:T(8,128)(2,1)} %copy.244), channel_id=1, source_target_pairs={{0,1},{1,2},{2,3},{3,4},{4,5},{5,6},{6,7},{7,0}} | collective-permute-start | bytes 4718600 | tf_op jit(solution)/shard_map/while/body/eval_jaxpr/ppermute | solution.py:110
  5861.8 458.9 %collective-permute-start.4 = (f32[768,8,128]{2,0,1:T(8,128)}, f32[768,8,128]{2,0,1:T(8,128)S(1)}, u32[]{:S(2)}, u32[]{:S(2)}) collective-permute-start(f32[768,8,128]{2,0,1:T(8,128)} %get-tuple-element.1176), channel_id=1, source_target_pairs={{0,1},{1,2},{2,3},{3,4},{4,5},{5,6},{6,7},{7,0}} | collective-permute-start | bytes 9437192 | tf_op jit(solution)/shard_map/while/body/eval_jaxpr/ppermute | solution.py:111
  5861.8 492.6 %collective-permute-start.5 = (f32[768,8,128]{2,0,1:T(8,128)}, f32[768,8,128]{2,0,1:T(8,128)}, u32[]{:S(2)}, u32[]{:S(2)}) collective-permute-start(f32[768,8,128]{2,0,1:T(8,128)} %get-tuple-element.1177), channel_id=1, source_target_pairs={{0,1},{1,2},{2,3},{3,4},{4,5},{5,6},{6,7},{7,0}} | collective-permute-start | bytes 9437192 | tf_op jit(solution)/shard_map/while/body/eval_jaxpr/ppermute | solution.py:112
  5861.8 509.4 %collective-permute-start.2 = (bf16[768,8,128]{2,0,1:T(8,128)(2,1)}, bf16[768,8,128]{2,0,1:T(8,128)(2,1)}, u32[]{:S(2)}, u32[]{:S(2)}) collective-permute-start(bf16[768,8,128]{2,0,1:T(8,128)(2,1)} %copy.243), channel_id=1, source_target_pairs={{0,1},{1,2},{2,3},{3,4},{4,5},{5,6},{6,7},{7,0}} | collective-permute-start | bytes 4718600 | tf_op jit(solution)/shard_map/while/body/eval_jaxpr/ppermute | solution.py:109
  5861.9 526.3 %collective-permute-start.3 = (bf16[768,8,128]{2,0,1:T(8,128)(2,1)}, bf16[768,8,128]{2,0,1:T(8,128)(2,1)}, u32[]{:S(2)}, u32[]{:S(2)}) collective-permute-start(bf16[768,8,128]{2,0,1:T(8,128)(2,1)} %copy.244), channel_id=1, source_target_pairs={{0,1},{1,2},{2,3},{3,4},{4,5},{5,6},{6,7},{7,0}} | collective-permute-start | bytes 4718600 | tf_op jit(solution)/shard_map/while/body/eval_jaxpr/ppermute | solution.py:110
  6411.1 670.3 %all-reduce.7.cloned.1.call-start = ((), (), s32[]{:S(2)}) async-start(), calls=%async_computation.2 | async-start | bytes 8388608 | tf_op jit(solution)/shard_map/psum | solution.py:124
  (75 other events, 11699.7 us)
Sparse Core Ops, SparseCore 0:
  36.4 69.1 all-gather.2
  6411.2 556.3 reduce-scatter.1
  6992.1 85.5 all-reduce.6
where the time goes:
time: 7120 us; the launch traced here: 7100 us
  waiting for transfers between devices  3940 us (55%)
  starting transfers between devices  2000 us (28%)
  local copies, waits for them, and re-layouts  818 us (11%)
  matrix products  161 us (2%)
    ppermute x7, waiting for transfers between devices, bwd_step(): dk_acc = lax.ppermute(dk_acc, 'cp', shift_pairs)  1900 us
    ppermute x7, waiting for transfers between devices, fwd_step(): k_blk = lax.ppermute(k_blk, 'cp', shift_pairs)  900 us
    ppermute x7, starting transfers between devices, bwd_step(): k_blk = lax.ppermute(k_blk, 'cp', shift_pairs)  698 us
    reduce_scatter x1, waiting for transfers between devices, local_fn(): lax.psum_scatter(grad_rel, 'cp', scatter_dimension=0, tiled=False)  556 us
    ppermute x7, starting transfers between devices, bwd_step(): v_blk = lax.ppermute(v_blk, 'cp', shift_pairs)  380 us
    ppermute x7, starting transfers between devices, bwd_step(): dv_acc = lax.ppermute(dv_acc, 'cp', shift_pairs)  366 us
    ppermute x7, starting transfers between devices, fwd_step(): v_blk = lax.ppermute(v_blk, 'cp', shift_pairs)  282 us
    ppermute x7, starting transfers between devices, fwd_step(): k_blk = lax.ppermute(k_blk, 'cp', shift_pairs)  275 us
  transfers between devices with their start and end apart: 47, of which 42 were waited for; matrix products, arithmetic and copies ran while one was open for 6% of the time, Pallas kernels for 0%

commit v1 on v0

v1 whole, which is shorter than its diff:
```python
import functools
import jax
import jax.numpy as jnp
from jax import lax
from jax.experimental import pallas as pl
from jax.experimental.pallas import tpu as pltpu
from jax.sharding import PartitionSpec as P

TILE = 256
BLK = 128
LOG2E = 1.4426950408889634


def dot_nt(lhs, rhs):
    return lax.dot_general(lhs, rhs, (((1,), (1,)), ((), ())), preferred_element_type=jnp.float32)


def dot_nn(lhs, rhs):
    return lax.dot_general(lhs, rhs, (((1,), (0,)), ((), ())), preferred_element_type=jnp.float32)


def head_kernel(x_hbm, u_ref, w_ref, y_ref, sums_ref,
                q_s, k_s, v_s, g_s, r_s, score_s, roll_s, ds_s, out_s, gu_s, gv_s, max_s, sum_s,
                qv_s, qu_s, quT_s, qvT_s, gT_s, dk_s, dv_s, dr_s, in_sem):
    n_src, _, rows, dim = x_hbm.shape
    n_tiles = n_src * rows // TILE
    nb = TILE // BLK
    inv_sqrt = dim ** -0.5
    scale2 = inv_sqrt * LOG2E
    bf16 = jnp.bfloat16
    f32 = jnp.float32

    copies = []
    for src in range(n_src):
        for arr, dst in enumerate((q_s, k_s, v_s, g_s, r_s)):
            copies.append(pltpu.make_async_copy(x_hbm.at[src, arr], dst.at[pl.ds(src * rows, rows)], in_sem.at[src, arr]))
    for copy in copies:
        copy.start()
    for copy in copies:
        copy.wait()

    sums_ref[...] = jnp.zeros_like(sums_ref)
    dk_s[...] = jnp.zeros_like(dk_s)
    dv_s[...] = jnp.zeros_like(dv_s)
    dr_s[...] = jnp.zeros_like(dr_s)

    row_id = lax.broadcasted_iota(jnp.int32, (BLK, BLK), 0)
    col_id = lax.broadcasted_iota(jnp.int32, (BLK, BLK), 1)
    low = col_id <= row_id

    def tile_rows(ref, idx):
        return ref[pl.ds(pl.multiple_of(idx * TILE, TILE), TILE), :]

    def blk(ref, slot, h, u):
        return ref[slot, pl.ds(h * BLK, BLK), pl.ds(u * BLK, BLK)]

    def by_off(ref, cur, prev, h, d):
        return blk(ref, cur, h, d) if d >= 0 else blk(ref, prev, h, d + nb)

    back_idx = lax.rem(col_id + row_id + 1, BLK)

    def unroll_blk(x):
        return jnp.take_along_axis(x, back_idx, axis=1)

    @pl.loop(0, n_tiles)
    def _(i):
        q_wide = tile_rows(q_s, i).astype(f32)
        qu_f = q_wide + u_ref[...]
        qv_f = q_wide + w_ref[...]
        qu_s[...] = qu_f.astype(bf16)
        qv_s[...] = qv_f.astype(bf16)
        quT_s[...] = qu_f.T.astype(bf16)
        qvT_s[...] = qv_f.T.astype(bf16)
        g_tile = tile_rows(g_s, i)
        gT_s[...] = g_tile.astype(f32).T.astype(bf16)
        max_s[...] = jnp.full_like(max_s, -jnp.inf)
        sum_s[...] = jnp.zeros_like(sum_s)
        out_s[...] = jnp.zeros_like(out_s)
        gu_s[...] = jnp.zeros_like(gu_s)
        gv_s[...] = jnp.zeros_like(gv_s)

        def score_step(m, diag):
            kt = i - m
            cur = lax.rem(m, 2)
            prev = 1 - cur
            by_offset = dot_nt(qv_s[...], tile_rows(r_s, m))
            for h in range(nb):
                for d in range(nb):
                    piece = by_offset[h * BLK:(h + 1) * BLK, d * BLK:(d + 1) * BLK]
                    roll_s[cur, pl.ds(h * BLK, BLK), pl.ds(d * BLK, BLK)] = pltpu.roll(piece, 1, 1, stride=1, stride_axis=0)
            content = dot_nt(qu_s[...], tile_rows(k_s, kt))
            for h in range(nb):
                top = max_s[pl.ds(h * BLK, BLK), :]
                for u in range(nb):
                    piece = content[h * BLK:(h + 1) * BLK, u * BLK:(u + 1) * BLK]
                    if diag and u > h:
                        s_blk = jnp.full((BLK, BLK), -jnp.inf, f32)
                    elif diag and u == h:
                        s_blk = jnp.where(low, piece + by_off(roll_s, cur, prev, h, 0), -jnp.inf)
                    else:
                        s_blk = piece + jnp.where(low, by_off(roll_s, cur, prev, h, h - u), by_off(roll_s, cur, prev, h, h - u - 1))
                    score_s[kt, pl.ds(h * BLK, BLK), pl.ds(u * BLK, BLK)] = s_blk
                    top = jnp.maximum(top, s_blk)
                max_s[pl.ds(h * BLK, BLK), :] = top

        score_step(0, True)

        @pl.loop(1, i + 1)
        def _(m):
            score_step(m, False)

        row_max = jnp.max(max_s[...], axis=1, keepdims=True) * scale2

        @pl.loop(0, i + 1)
        def _(kt):
            prob = jnp.exp2(score_s[kt] * scale2 - row_max)
            score_s[kt] = prob
            part = prob[:, :BLK]
            for u in range(1, nb):
                part = part + prob[:, u * BLK:(u + 1) * BLK]
            sum_s[...] += part
            out_s[...] += dot_nn(prob.astype(bf16), tile_rows(v_s, kt))

        inv_sum = 1.0 / jnp.sum(sum_s[...], axis=1, keepdims=True)
        out = out_s[...] * inv_sum
        delta = jnp.sum(out * g_tile.astype(f32), axis=1, keepdims=True)
        per = rows // TILE
        c_idx = i // per
        r_idx = pl.multiple_of(lax.rem(i, per) * TILE, TILE)
        y_ref[c_idx, 0, pl.ds(r_idx, TILE), :] = out.astype(bf16)
        ds_s[1] = jnp.zeros((TILE, TILE), f32)

        @pl.loop(0, i + 1)
        def _(kt):
            m = i - kt
            cur = lax.rem(kt, 2)
            prev = 1 - cur
            d_prob = dot_nt(tile_rows(g_s, i), tile_rows(v_s, kt))
            prob = score_s[kt] * inv_sum
            d_score = prob * (d_prob - delta)
            ds_s[cur] = d_score
            prob_b = prob.astype(bf16)
            ds_b = d_score.astype(bf16)
            dv_s[kt] += dot_nn(gT_s[...], prob_b)
            dk_s[kt] += dot_nn(quT_s[...], ds_b)
            gu_s[...] += dot_nn(ds_b, tile_rows(k_s, kt))
            out_rows = []
            for h in range(nb):
                cols = []
                for d in range(nb):
                    near = by_off(ds_s, cur, prev, h, h - d)
                    far = by_off(ds_s, cur, prev, h, h - d - 1)
                    cols.append(unroll_blk(jnp.where(low, near, far)))
                out_rows.append(jnp.concatenate(cols, axis=1))
            wide = jnp.concatenate(out_rows, axis=0).astype(bf16)
            gv_s[...] += dot_nn(wide, tile_rows(r_s, m))
            dr_s[m] += dot_nn(qvT_s[...], wide)

        gu = gu_s[...] * inv_sqrt
        gv = gv_s[...] * inv_sqrt
        y_ref[c_idx, 1, pl.ds(r_idx, TILE), :] = (gu + gv).astype(bf16)
        sums_ref[0:1, :] += jnp.sum(gu, axis=0, keepdims=True)
        sums_ref[1:2, :] += jnp.sum(gv, axis=0, keepdims=True)

    @pl.loop(0, n_tiles)
    def _(t):
        per = rows // TILE
        c_idx = t // per
        r_idx = pl.multiple_of(lax.rem(t, per) * TILE, TILE)
        y_ref[c_idx, 2, pl.ds(r_idx, TILE), :] = (dk_s[t] * inv_sqrt).T.astype(bf16)
        y_ref[c_idx, 3, pl.ds(r_idx, TILE), :] = dv_s[t].T.astype(bf16)
        y_ref[c_idx, 4, pl.ds(r_idx, TILE), :] = (dr_s[t] * inv_sqrt).T.astype(bf16)


def run_head(x, u_row, v_row):
    n_src, n_arr, rows, dim = x.shape
    seq = n_src * rows
    n_tiles = seq // TILE
    bf16 = jnp.bfloat16
    f32 = jnp.float32
    vmem = pl.BlockSpec(memory_space=pltpu.VMEM)
    tall = pltpu.VMEM((seq, dim), bf16)
    return pl.pallas_call(
        head_kernel,
        out_shape=(jax.ShapeDtypeStruct((n_src, n_arr, rows, dim), bf16), jax.ShapeDtypeStruct((8, dim), f32)),
        in_specs=[pl.BlockSpec(memory_space=pl.ANY), vmem, vmem],
        out_specs=(vmem, vmem),
        scratch_shapes=[
            tall, tall, tall, tall, tall,
            pltpu.VMEM((n_tiles, TILE, TILE), f32),
            pltpu.VMEM((2, TILE, TILE), f32),
            pltpu.VMEM((2, TILE, TILE), f32),
            pltpu.VMEM((TILE, dim), f32),
            pltpu.VMEM((TILE, dim), f32),
            pltpu.VMEM((TILE, dim), f32),
            pltpu.VMEM((TILE, BLK), f32),
            pltpu.VMEM((TILE, BLK), f32),
            pltpu.VMEM((TILE, dim), bf16),
            pltpu.VMEM((TILE, dim), bf16),
            pltpu.VMEM((dim, TILE), bf16),
            pltpu.VMEM((dim, TILE), bf16),
            pltpu.VMEM((dim, TILE), bf16),
            pltpu.VMEM((n_tiles, dim, TILE), f32),
            pltpu.VMEM((n_tiles, dim, TILE), f32),
            pltpu.VMEM((n_tiles, dim, TILE), f32),
            pltpu.SemaphoreType.DMA((n_src, n_arr)),
        ],
        compiler_params=pltpu.CompilerParams(vmem_limit_bytes=60 * 1024 * 1024),
        cost_estimate=pl.CostEstimate(flops=9 * seq * seq * dim, bytes_accessed=4 * seq * n_arr * dim, transcendentals=seq * seq // 2),
        name='rel_attention_head',
    )(x, u_row, v_row)


def solution(mesh):
    seq_spec = P('cp', 'hp', None)
    head_spec = P('hp', None)
    weight_spec = P(None, 'hp', None)

    def local_fn(q, k, v, u_bias, v_bias, rel_table, w_rel, d_out):
        block_len, num_heads, head_dim = q.shape
        model_dim = rel_table.shape[1]
        f32 = jnp.float32
        bf16 = jnp.bfloat16
        me = lax.axis_index('cp')
        flipped = rel_table.reshape(block_len // BLK, BLK, model_dim)[:, ::-1].reshape(block_len, model_dim)
        table_all = lax.all_gather(flipped, 'cp', axis=0, tiled=True)
        rel_mine = jnp.dot(flipped, w_rel.reshape(model_dim, num_heads * head_dim), preferred_element_type=f32)
        rel_mine = rel_mine.astype(bf16).reshape(block_len, num_heads, head_dim)
        packed = jnp.stack([q, k, v, d_out, rel_mine], axis=0).transpose(2, 0, 1, 3)
        arrived = lax.all_to_all(packed, 'cp', 0, 0, tiled=True)
        u_row = lax.dynamic_slice_in_dim(u_bias, me, 1, 0)
        v_row = lax.dynamic_slice_in_dim(v_bias, me, 1, 0)
        y, sums = run_head(arrived, u_row, v_row)
        d_rel = y[:, 4].reshape(-1, head_dim)
        back = lax.all_to_all(y[:, :4], 'cp', 0, 0, tiled=True)
        back = back.transpose(1, 2, 0, 3)
        d_w = lax.dot_general(table_all, d_rel, (((0,), (0,)), ((), ())), preferred_element_type=f32)
        tail = lax.all_gather(jnp.concatenate([d_w, sums], axis=0), 'cp')
        d_w_rel = tail[:, :model_dim].transpose(1, 0, 2)
        return back[0], back[1], back[2], back[3], tail[:, model_dim], tail[:, model_dim + 1], d_w_rel

    return jax.shard_map(
        local_fn,
        mesh=mesh,
        in_specs=(seq_spec, seq_spec, seq_spec, head_spec, head_spec, P('cp', None), weight_spec, seq_spec),
        out_specs=(seq_spec, seq_spec, seq_spec, seq_spec, head_spec, head_spec, weight_spec),
        check_vma=False,
    )
```

time: 7120 us -> 655 us (0.09)
  waiting for transfers between devices: 3940 us -> 125 us
  starting transfers between devices: 2000 us -> 4.38 us
  local copies, waits for them, and re-layouts: 818 us -> 60.7 us
  Pallas kernels: 0 us -> 348 us
  matrix products: 161 us -> 10.9 us
    ppermute x44 -> x0, waiting for transfers between devices: 3330 us -> none  [the longest x7 1900 us: bwd_step(): dk_acc = lax.ppermute(dk_acc, 'cp', shift_pairs)]
    ppermute x44 -> x0, starting transfers between devices: 2000 us -> none  [the longest x7 698 us: bwd_step(): k_blk = lax.ppermute(k_blk, 'cp', shift_pairs)]
    reduce_scatter x1 -> x0, waiting for transfers between devices: 556 us -> none  [local_fn(): lax.psum_scatter(grad_rel, 'cp', scatter_dimension=0, tiled=False)]
    pallas_call x0 -> x1, Pallas kernels: none -> 348 us  [run_head(): pl.pallas_call(head_kernel, out_shape=(jax.ShapeDtypeStruct((n_src, n_arr...]
    cond x26 -> x0, local copies, waits for them, and re-layouts: 248 us -> none
    reshape x3 -> x0, local copies, waits for them, and re-layouts: 151 us -> none  [the longest x2 118 us: skew_scores(): kept_view.reshape(lead_dims + (block_len, 2 * block_len - 1))]
    dot_general x13 -> x2, matrix products: 161 us -> 10.9 us  [the longest x1 6.39 us: local_fn(): lax.dot_general(table_all, d_rel, (((0,), (0,)), ((), ())), preferred_ele...]
    all_to_all x0 -> x1, waiting for transfers between devices: none -> 125 us  [local_fn(): arrived = lax.all_to_all(packed, 'cp', 0, 0, tiled=True)]
  transfers between devices with their start and end apart: 47 -> 3, of which waited for: 42 -> 1; matrix products, arithmetic and copies ran while one was open for 6% -> 4% of each run, Pallas kernels for 0% -> 53%
where the time goes in v1:
time: 655 us; the launch traced here: 652 us
  Pallas kernels  348 us (53%)
  waiting for transfers between devices  125 us (19%)
  blocking collectives  88.6 us (14%)
  local copies, waits for them, and re-layouts  60.7 us (9%)
  between operations  14.2 us (2%)
  matrix products  10.9 us (2%)
    pallas_call x1, Pallas kernels, run_head(): pl.pallas_call(head_kernel, out_shape=(jax.ShapeDtypeStruct((n_src, n_arr...  348 us
    all_to_all x1, waiting for transfers between devices, local_fn(): arrived = lax.all_to_all(packed, 'cp', 0, 0, tiled=True)  125 us
    all_to_all x1, blocking collectives, local_fn(): back = lax.all_to_all(y[:, :4], 'cp', 0, 0, tiled=True)  88.6 us
    rev x1, local copies, waits for them, and re-layouts, local_fn(): rel_table.reshape(block_len // BLK, BLK, model_dim)[:, ::-1]  23.1 us
    unnamed x19, local copies, waits for them, and re-layouts  22.5 us
  transfers between devices with their start and end apart: 3, of which 1 were waited for; matrix products, arithmetic and copies ran while one was open for 4% of the time, Pallas kernels for 53%

profile of v1, /device:TPU:0, one launch (start us, length us, event | category | flops | bytes accessed | tf_op | source)
XLA Modules:
  0.0 651.9 jit_solution(12194946044860815557)
XLA Ops:
  7.2 23.1 %rev.3 = bf16[6,128,1024]{2,1,0:T(8,128)(2,1)} reverse(bf16[6,128,1024]{2,1,0:T(8,128)(2,1)} %bitcast.46), dimensions={1} | reverse | bytes 3145728 | tf_op jit(solution)/shard_map/rev | solution.py:225
  30.3 1.4 copy-done.1
  31.7 4.5 fusion.3
  36.2 1.7 copy.44
  38.8 1.7 bitcast_dynamic-update-slice_fusion.3
  41.1 1.1 copy-done.3
  42.5 1.1 copy-done.4
  44.1 3.0 copy-done
  47.1 4.3 all-to-all-start
  51.5 1.2 constant_dynamic-slice_fusion
  52.7 125.0 %all-to-all-done.x_hbm = bf16[8,5,768,128]{3,2,1,0:T(8,128)(2,1)} async-done(((bf16[8,5,768,128]{3,2,1,0:T(8,128)(2,1)}), bf16[8,5,768,128]{3,2,1,0:T(8,128)(2,1)}, u32[]{:S(2)}, u32[]{:S(2)}) %all-to-all-start) | async-done | bytes 7864352 | tf_op jit(solution)/shard_map/all_to_all | solution.py:230
  177.7 347.9 %rel_attention_head.1 = (bf16[8,5,768,128]{3,2,1,0:T(8,128)(2,1)}, f32[8,128]{1,0:T(8,128)}) custom-call(bf16[8,5,768,128]{3,2,1,0:T(8,128)(2,1)} %all-to-all-done.x_hbm, f32[1,128]{1,0:T(1,128)} %get-tuple-element.39.u_ref, f32[1,128]{1,0:T(1,128)} %get-tuple-element.38.w_ref), custom_call_target="tpu_custom_call" | custom-call | flops 43486543872 | bytes 15728640 | tf_op jit(solution)/shard_map/rel_attention_head/pallas_call | solution.py:183
  526.4 1.5 slice.32
  528.0 6.4 convolution_bitcast_fusion
  534.4 1.0 copy.47
  535.5 3.2 slice.27
  538.7 88.6 %all_to_all.10 = bf16[8,4,768,128]{3,2,1,0:T(8,128)(2,1)S(1)} all-to-all(bf16[8,4,768,128]{3,2,1,0:T(8,128)(2,1)S(1)} %slice.27), channel_id=1, replica_groups=mesh['hp'=1,'cp'=8] {'cp'}, dimensions={0} | all-to-all | bytes 12582912 | tf_op jit(solution)/shard_map/all_to_all | solution.py:235
  628.0 2.2 copy.48
  630.2 2.2 copy.49
  632.3 2.2 copy.50
  634.5 2.2 copy.51
  636.6 1.4 fusion.6
  638.1 2.5 slice_bitcast_fusion
  640.6 4.4 copy.52
  (20 shorter events, 3.9 us)
Async XLA Ops:
  7.2 520.8 %all-gather.4.cloned.1.call-start = ((), (), s32[]{:S(2)}) async-start(), calls=%async_computation.2 | async-start | bytes 14155776 | tf_op jit(solution)/shard_map/all_gather | solution.py:226
  30.3 1.4 copy-start.1
  38.8 1.9 copy-start.2
  40.7 1.4 copy-start.3
  42.1 1.4 copy-start.4
  44.1 3.1 copy-start
  47.1 130.6 %all-to-all-start = ((bf16[8,5,768,128]{3,2,1,0:T(8,128)(2,1)}), bf16[8,5,768,128]{3,2,1,0:T(8,128)(2,1)}, u32[]{:S(2)}, u32[]{:S(2)}) async-start(bf16[8,5,768,128]{3,2,1,0:T(8,128)(2,1)} %bitcast.39), calls=%async_computation | async-start | bytes 15728640 | tf_op jit(solution)/shard_map/all_to_all | solution.py:230
  51.5 585.2 %all-gather.6.cloned.1.call-start = ((), (), s32[]{:S(2)}) async-start(), calls=%async_computation.3 | async-start | bytes 4755456 | tf_op jit(solution)/shard_map/all_gather | solution.py:238
Sparse Core Ops, SparseCore 0:
  30.4 128.7 all-gather.3
  535.6 64.4 all-gather.5

commit v2 on v1

--- a/solution.py
+++ b/solution.py
@@ -6,7 +6,7 @@
 from jax.experimental.pallas import tpu as pltpu
 from jax.sharding import PartitionSpec as P
 
-TILE = 256
+TILE = 768
 BLK = 128
 LOG2E = 1.4426950408889634
 
@@ -19,9 +19,10 @@
     return lax.dot_general(lhs, rhs, (((1,), (0,)), ((), ())), preferred_element_type=jnp.float32)
 
 
-def head_kernel(x_hbm, u_ref, w_ref, y_ref, sums_ref,
+def head_kernel(x_hbm, u_ref, w_ref, y_hbm, drel_ref, sums_ref,
                 q_s, k_s, v_s, g_s, r_s, score_s, roll_s, ds_s, out_s, gu_s, gv_s, max_s, sum_s,
-                qv_s, qu_s, quT_s, qvT_s, gT_s, dk_s, dv_s, dr_s, in_sem):
+                qv_s, qu_s, quT_s, qvT_s, gT_s, dk_s, dv_s, dr_s, stage_s,
+                in_send, in_recv, out_send, out_recv):
     n_src, _, rows, dim = x_hbm.shape
     n_tiles = n_src * rows // TILE
     nb = TILE // BLK
@@ -30,14 +31,48 @@
     bf16 = jnp.bfloat16
     f32 = jnp.float32
 
-    copies = []
-    for src in range(n_src):
-        for arr, dst in enumerate((q_s, k_s, v_s, g_s, r_s)):
-            copies.append(pltpu.make_async_copy(x_hbm.at[src, arr], dst.at[pl.ds(src * rows, rows)], in_sem.at[src, arr]))
-    for copy in copies:
-        copy.start()
-    for copy in copies:
-        copy.wait()
+    me = lax.axis_index('cp')
+    n_dev = n_src
+    arrays = (q_s, k_s, v_s, g_s, r_s)
+
+    def arrive(arr, src):
+        rows_of = arrays[arr].at[pl.ds(pl.multiple_of(src * rows, rows), rows)]
+        return pltpu.make_async_copy(x_hbm.at[me, arr], rows_of, in_recv.at[arr, src])
+
+    def depart(arr, dest):
+        return pltpu.make_async_remote_copy(
+            src_ref=x_hbm.at[dest, arr],
+            dst_ref=arrays[arr].at[pl.ds(pl.multiple_of(me * rows, rows), rows)],
+            send_sem=in_send.at[arr, dest], recv_sem=in_recv.at[arr, me],
+            device_id={'cp': dest}, device_id_type=pl.DeviceIdType.MESH)
+
+    def give(arr, dest):
+        return pltpu.make_async_remote_copy(
+            src_ref=stage_s.at[arr, dest], dst_ref=y_hbm.at[me, arr],
+            send_sem=out_send.at[arr, dest], recv_sem=out_recv.at[arr, me],
+            device_id={'cp': dest}, device_id_type=pl.DeviceIdType.MESH)
+
+    def keep(arr, src):
+        return pltpu.make_async_copy(stage_s.at[arr, me], y_hbm.at[src, arr], out_recv.at[arr, src])
+
+    def hand_out(arr, dest):
+        @pl.when(dest != me)
+        def _():
+            give(arr, dest).start()
+
+        @pl.when(dest == me)
+        def _():
+            keep(arr, me).start()
+
+    barrier = pltpu.get_barrier_semaphore()
+    for step in range(1, n_dev):
+        pl.semaphore_signal(barrier, inc=1, device_id={'cp': lax.rem(me + step, n_dev)}, device_id_type=pl.DeviceIdType.MESH)
+    pl.semaphore_wait(barrier, n_dev - 1)
+    order = (1, 0, 4, 2, 3)
+    for arr in order:
+        for step in range(1, n_dev):
+            depart(arr, lax.rem(me + step, n_dev)).start()
+        arrive(arr, me).start()
 
     sums_ref[...] = jnp.zeros_like(sums_ref)
     dk_s[...] = jnp.zeros_like(dk_s)
@@ -57,6 +92,8 @@
     def by_off(ref, cur, prev, h, d):
         return blk(ref, cur, h, d) if d >= 0 else blk(ref, prev, h, d + nb)
 
+    flip = jnp.where(row_id + col_id == BLK - 1, 1.0, 0.0).astype(bf16)
+
     back_idx = lax.rem(col_id + row_id + 1, BLK)
 
     def unroll_blk(x):
@@ -64,6 +101,11 @@
 
     @pl.loop(0, n_tiles)
     def _(i):
+        for arr in order[:3]:
+            arrive(arr, i).wait()
+        for b in range(nb):
+            here = pl.ds(pl.multiple_of(i * TILE + b * BLK, BLK), BLK)
+            r_s[here, :] = dot_nn(flip, r_s[here, :]).astype(bf16)
         q_wide = tile_rows(q_s, i).astype(f32)
         qu_f = q_wide + u_ref[...]
         qv_f = q_wide + w_ref[...]
@@ -71,8 +113,6 @@
         qv_s[...] = qv_f.astype(bf16)
         quT_s[...] = qu_f.T.astype(bf16)
         qvT_s[...] = qv_f.T.astype(bf16)
-        g_tile = tile_rows(g_s, i)
-        gT_s[...] = g_tile.astype(f32).T.astype(bf16)
         max_s[...] = jnp.full_like(max_s, -jnp.inf)
         sum_s[...] = jnp.zeros_like(sum_s)
         out_s[...] = jnp.zeros_like(out_s)
@@ -109,6 +149,7 @@
         def _(m):
             score_step(m, False)
 
+        arrive(2, i).wait()
         row_max = jnp.max(max_s[...], axis=1, keepdims=True) * scale2
 
         @pl.loop(0, i + 1)
@@ -121,13 +162,18 @@
             sum_s[...] += part
             out_s[...] += dot_nn(prob.astype(bf16), tile_rows(v_s, kt))
 
+        arrive(3, i).wait()
+        g_tile = tile_rows(g_s, i)
+        gT_s[...] = g_tile.astype(f32).T.astype(bf16)
         inv_sum = 1.0 / jnp.sum(sum_s[...], axis=1, keepdims=True)
         out = out_s[...] * inv_sum
         delta = jnp.sum(out * g_tile.astype(f32), axis=1, keepdims=True)
-        per = rows // TILE
-        c_idx = i // per
-        r_idx = pl.multiple_of(lax.rem(i, per) * TILE, TILE)
-        y_ref[c_idx, 0, pl.ds(r_idx, TILE), :] = out.astype(bf16)
+        stage_s[0, i] = out.astype(bf16)
+
+        @pl.when(i > 0)
+        def _():
+            hand_out(1, i - 1)
+
         ds_s[1] = jnp.zeros((TILE, TILE), f32)
 
         @pl.loop(0, i + 1)
@@ -156,20 +202,39 @@
             gv_s[...] += dot_nn(wide, tile_rows(r_s, m))
             dr_s[m] += dot_nn(qvT_s[...], wide)
 
+            @pl.when(i == n_tiles - 1)
+            def _():
+                stage_s[2, kt] = (dk_s[kt] * inv_sqrt).T.astype(bf16)
+                stage_s[3, kt] = dv_s[kt].T.astype(bf16)
+
+                @pl.when(kt > 0)
+                def _():
+                    hand_out(2, kt - 1)
+                    hand_out(3, kt - 1)
+
+        hand_out(0, i)
         gu = gu_s[...] * inv_sqrt
         gv = gv_s[...] * inv_sqrt
-        y_ref[c_idx, 1, pl.ds(r_idx, TILE), :] = (gu + gv).astype(bf16)
+        stage_s[1, i] = (gu + gv).astype(bf16)
         sums_ref[0:1, :] += jnp.sum(gu, axis=0, keepdims=True)
         sums_ref[1:2, :] += jnp.sum(gv, axis=0, keepdims=True)
 
-    @pl.loop(0, n_tiles)
-    def _(t):
-        per = rows // TILE
-        c_idx = t // per
-        r_idx = pl.multiple_of(lax.rem(t, per) * TILE, TILE)
-        y_ref[c_idx, 2, pl.ds(r_idx, TILE), :] = (dk_s[t] * inv_sqrt).T.astype(bf16)
-        y_ref[c_idx, 3, pl.ds(r_idx, TILE), :] = dv_s[t].T.astype(bf16)
-        y_ref[c_idx, 4, pl.ds(r_idx, TILE), :] = (dr_s[t] * inv_sqrt).T.astype(bf16)
+    hand_out(2, n_tiles - 1)
+    hand_out(3, n_tiles - 1)
+    for t in range(n_tiles):
+        d_rel = (dr_s[t] * inv_sqrt).T.astype(bf16)
+        for b in range(nb):
+            drel_ref[pl.ds(t * TILE + b * BLK, BLK), :] = dot_nn(flip, d_rel[b * BLK:(b + 1) * BLK]).astype(bf16)
+    hand_out(1, n_tiles - 1)
+    for step in range(1, n_dev):
+        dest = lax.rem(me + step, n_dev)
+        for arr in range(5):
+            depart(arr, dest).wait_send()
+        for arr in range(4):
+            give(arr, dest).wait_send()
+    for src in range(n_dev):
+        for arr in range(4):
+            keep(arr, src).wait()
 
 
 def run_head(x, u_row, v_row):
@@ -182,9 +247,9 @@
     tall = pltpu.VMEM((seq, dim), bf16)
     return pl.pallas_call(
         head_kernel,
-        out_shape=(jax.ShapeDtypeStruct((n_src, n_arr, rows, dim), bf16), jax.ShapeDtypeStruct((8, dim), f32)),
+        out_shape=(jax.ShapeDtypeStruct((n_src, 4, rows, dim), bf16), jax.ShapeDtypeStruct((seq, dim), bf16), jax.ShapeDtypeStruct((8, dim), f32)),
         in_specs=[pl.BlockSpec(memory_space=pl.ANY), vmem, vmem],
-        out_specs=(vmem, vmem),
+        out_specs=(pl.BlockSpec(memory_space=pl.ANY), vmem, vmem),
         scratch_shapes=[
             tall, tall, tall, tall, tall,
             pltpu.VMEM((n_tiles, TILE, TILE), f32),
@@ -203,9 +268,13 @@
             pltpu.VMEM((n_tiles, dim, TILE), f32),
             pltpu.VMEM((n_tiles, dim, TILE), f32),
             pltpu.VMEM((n_tiles, dim, TILE), f32),
-            pltpu.SemaphoreType.DMA((n_src, n_arr)),
+            pltpu.VMEM((4, n_src, rows, dim), bf16),
+            pltpu.SemaphoreType.DMA((n_arr, n_src)),
+            pltpu.SemaphoreType.DMA((n_arr, n_src)),
+            pltpu.SemaphoreType.DMA((4, n_src)),
+            pltpu.SemaphoreType.DMA((4, n_src)),
         ],
-        compiler_params=pltpu.CompilerParams(vmem_limit_bytes=60 * 1024 * 1024),
+        compiler_params=pltpu.CompilerParams(vmem_limit_bytes=60 * 1024 * 1024, collective_id=0, has_side_effects=True),
         cost_estimate=pl.CostEstimate(flops=9 * seq * seq * dim, bytes_accessed=4 * seq * n_arr * dim, transcendentals=seq * seq // 2),
         name='rel_attention_head',
     )(x, u_row, v_row)
@@ -222,18 +291,14 @@
         f32 = jnp.float32
         bf16 = jnp.bfloat16
         me = lax.axis_index('cp')
-        flipped = rel_table.reshape(block_len // BLK, BLK, model_dim)[:, ::-1].reshape(block_len, model_dim)
-        table_all = lax.all_gather(flipped, 'cp', axis=0, tiled=True)
-        rel_mine = jnp.dot(flipped, w_rel.reshape(model_dim, num_heads * head_dim), preferred_element_type=f32)
+        table_all = lax.all_gather(rel_table, 'cp', axis=0, tiled=True)
+        rel_mine = jnp.dot(rel_table, w_rel.reshape(model_dim, num_heads * head_dim), preferred_element_type=f32)
         rel_mine = rel_mine.astype(bf16).reshape(block_len, num_heads, head_dim)
         packed = jnp.stack([q, k, v, d_out, rel_mine], axis=0).transpose(2, 0, 1, 3)
-        arrived = lax.all_to_all(packed, 'cp', 0, 0, tiled=True)
         u_row = lax.dynamic_slice_in_dim(u_bias, me, 1, 0)
         v_row = lax.dynamic_slice_in_dim(v_bias, me, 1, 0)
-        y, sums = run_head(arrived, u_row, v_row)
-        d_rel = y[:, 4].reshape(-1, head_dim)
-        back = lax.all_to_all(y[:, :4], 'cp', 0, 0, tiled=True)
-        back = back.transpose(1, 2, 0, 3)
+        y, d_rel, sums = run_head(packed, u_row, v_row)
+        back = y.transpose(1, 2, 0, 3)
         d_w = lax.dot_general(table_all, d_rel, (((0,), (0,)), ((), ())), preferred_element_type=f32)
         tail = lax.all_gather(jnp.concatenate([d_w, sums], axis=0), 'cp')
         d_w_rel = tail[:, :model_dim].transpose(1, 0, 2)

time: 655 us -> 403 us (0.62)
  blocking collectives: 88.6 us -> 0 us
  waiting for transfers between devices: 125 us -> 48.9 us
  Pallas kernels: 348 us -> 293 us
  local copies, waits for them, and re-layouts: 60.7 us -> 34.8 us
    all_to_all x1 -> x0, waiting for transfers between devices: 125 us -> none  [local_fn(): arrived = lax.all_to_all(packed, 'cp', 0, 0, tiled=True)]
    all_to_all x1 -> x0, blocking collectives: 88.6 us -> none  [local_fn(): back = lax.all_to_all(y[:, :4], 'cp', 0, 0, tiled=True)]
    pallas_call x1, Pallas kernels: 348 us -> 293 us  [run_head(): pl.pallas_call(head_kernel, out_shape=(jax.ShapeDtypeStruct((n_src, 4, ro...]
    all_gather x1, waiting for transfers between devices: 0.01 us -> 48.2 us  [local_fn(): tail = lax.all_gather(jnp.concatenate([d_w, sums], axis=0), 'cp')]
    rev x1 -> x0, local copies, waits for them, and re-layouts: 23.1 us -> none  [local_fn(): rel_table.reshape(block_len // BLK, BLK, model_dim)[:, ::-1]]
  transfers between devices with their start and end apart: 3 -> 2, of which waited for: 1 -> 1; matrix products, arithmetic and copies ran while one was open for 4% -> 6% of each run, Pallas kernels for 53% -> 73%
where the time goes in v2:
time: 403 us; the launch traced here: 402 us
  Pallas kernels  293 us (73%)
  waiting for transfers between devices  48.9 us (12%)
  local copies, waits for them, and re-layouts  34.8 us (9%)
  between operations  14.2 us (4%)
  matrix products  11.4 us (3%)
    pallas_call x1, Pallas kernels, run_head(): pl.pallas_call(head_kernel, out_shape=(jax.ShapeDtypeStruct((n_src, 4, ro...  293 us
    all_gather x1, waiting for transfers between devices, local_fn(): tail = lax.all_gather(jnp.concatenate([d_w, sums], axis=0), 'cp')  48.2 us
    unnamed x19, local copies, waits for them, and re-layouts  21.8 us
  transfers between devices with their start and end apart: 2, of which 1 were waited for; matrix products, arithmetic and copies ran while one was open for 6% of the time, Pallas kernels for 73%

profile of v2, /device:TPU:0, one launch (start us, length us, event | category | flops | bytes accessed | tf_op | source)
XLA Modules:
  0.0 402.1 jit_solution(12391762713853772107)
XLA Ops:
  7.2 0.7 all-gather.4.cloned.1.call-update
  8.0 0.6 copy-done.3
  8.6 4.5 %fusion.3 = bf16[768,1024]{1,0:T(8,128)(2,1)} fusion(bf16[768,1024]{1,0:T(8,128)(2,1)S(1)} %copy-done.3, bf16[128,8,8,128]{3,2,1,0:T(8,128)(2,1)} %bitcast.42), kind=kOutput, calls=%fused_computation.4 | convolution fusion | flops 1611399168 | bytes 5242880 | tf_op jit(solution)/shard_map/dot_general | solution.py:295
  13.1 1.7 copy.44
  14.8 0.9 copy.45
  15.7 1.2 constant_dynamic-slice_fusion
  17.0 1.7 bitcast_dynamic-update-slice_fusion.3
  19.2 1.1 copy-done.1
  20.2 0.3 bitcast_dynamic-update-slice_fusion.1
  20.6 1.1 copy-done.2
  22.2 3.1 copy-done.4
  25.3 292.7 %rel_attention_head.1 = (bf16[8,4,768,128]{3,2,1,0:T(8,128)(2,1)}, bf16[6144,128]{1,0:T(8,128)(2,1)}, f32[8,128]{1,0:T(8,128)}) custom-call(bf16[8,5,768,128]{3,2,1,0:T(8,128)(2,1)} %bitcast.39, f32[1,128]{1,0:T(1,128)} %get-tuple-element.41.u_ref, f32[1,128]{1,0:T(1,128)} %get-tuple-element.40.w_ref), custom_call_target="tpu_custom_call" | custom-call | flops 43486543872 | bytes 15728640 | tf_op jit(solution)/shard_map/rel_attention_head/pallas_call | solution.py:248
  318.0 0.8 copy.46
  318.8 6.9 %convolution_bitcast_fusion = f32[1024,128]{0,1:T(8,128)S(1)} fusion(bf16[6144,128]{1,0:T(8,128)(2,1)} %get-tuple-element.11, bf16[6144,1024]{1,0:T(8,128)(2,1)} %all-gather.4.cloned.1.call-done), kind=kOutput, calls=%fused_computation.13 | convolution fusion | flops 1610612736 | bytes 14680064 | tf_op jit(solution)/shard_map/dot_general | solution.py:302
  325.7 1.0 copy.47
  326.8 3.3 slice_bitcast_fusion.1
  330.0 2.2 copy.48
  332.2 2.2 copy.49
  334.4 2.2 copy.50
  336.5 2.2 copy.51
  338.7 48.2 %all-gather.6.cloned.1.call-done = f32[8256,128]{1,0:T(8,128)} async-done(((f32[1032,128]{1,0:T(8,128)}), f32[8256,128]{1,0:T(8,128)}) %all-gather.6.cloned.1.call-update) | async-done | bytes 4227088 | tf_op jit(solution)/shard_map/all_gather | solution.py:303
  386.8 1.4 fusion.6
  388.3 2.5 slice_bitcast_fusion
  390.8 4.4 %copy.52 = f32[1024,8,128]{2,1,0:T(8,128)} copy(f32[1024,8,128]{2,0,1:T(8,128)S(1)} %slice_bitcast_fusion) | data formatting | bytes 8388608
  (14 shorter events, 1.2 us)
Async XLA Ops:
  7.2 1.4 copy-start.3
  7.2 311.6 %all-gather.4.cloned.1.call-start = ((), (), s32[]{:S(2)}) async-start(), calls=%async_computation | async-start | bytes 14155776 | tf_op jit(solution)/shard_map/all_gather | solution.py:294
  7.9 378.9 %all-gather.6.cloned.1.call-start = ((), (), s32[]{:S(2)}) async-start(), calls=%async_computation.1 | async-start | bytes 4755456 | tf_op jit(solution)/shard_map/all_gather | solution.py:303
  17.0 1.9 copy-start
  18.8 1.4 copy-start.1
  20.2 1.4 copy-start.2
  22.2 3.1 copy-start.4
Sparse Core Ops, SparseCore 0:
  9.8 148.8 all-gather.3
  326.9 59.9 all-gather.5

commit v3 on v2

--- a/solution.py
+++ b/solution.py
@@ -19,11 +19,16 @@
     return lax.dot_general(lhs, rhs, (((1,), (0,)), ((), ())), preferred_element_type=jnp.float32)
 
 
-def head_kernel(x_hbm, u_ref, w_ref, y_hbm, drel_ref, sums_ref,
+def head_kernel(xq_hbm, xk_hbm, xv_hbm, xg_hbm, xr_hbm, table_hbm, u_ref, w_ref,
+                yo_hbm, yq_hbm, yk_hbm, yv_hbm, tab_hbm, dw_hbm,
                 q_s, k_s, v_s, g_s, r_s, score_s, roll_s, ds_s, out_s, gu_s, gv_s, max_s, sum_s,
                 qv_s, qu_s, quT_s, qvT_s, gT_s, dk_s, dv_s, dr_s, stage_s,
-                in_send, in_recv, out_send, out_recv):
-    n_src, _, rows, dim = x_hbm.shape
+                sums_ref, tbuf_s, dwT_s, dw_s,
+                in_send, in_recv, out_send, out_recv, tab_send, tab_recv, dw_send, dw_recv, load_sem):
+    n_src, rows, dim = xq_hbm.shape
+    model_dim = table_hbm.shape[1]
+    x_hbm = (xq_hbm, xk_hbm, xv_hbm, xg_hbm, xr_hbm)
+    y_hbm = (yo_hbm, yq_hbm, yk_hbm, yv_hbm)
     n_tiles = n_src * rows // TILE
     nb = TILE // BLK
     inv_sqrt = dim ** -0.5
@@ -37,23 +42,23 @@
 
     def arrive(arr, src):
         rows_of = arrays[arr].at[pl.ds(pl.multiple_of(src * rows, rows), rows)]
-        return pltpu.make_async_copy(x_hbm.at[me, arr], rows_of, in_recv.at[arr, src])
+        return pltpu.make_async_copy(x_hbm[arr].at[me], rows_of, in_recv.at[arr, src])
 
     def depart(arr, dest):
         return pltpu.make_async_remote_copy(
-            src_ref=x_hbm.at[dest, arr],
+            src_ref=x_hbm[arr].at[dest],
             dst_ref=arrays[arr].at[pl.ds(pl.multiple_of(me * rows, rows), rows)],
             send_sem=in_send.at[arr, dest], recv_sem=in_recv.at[arr, me],
             device_id={'cp': dest}, device_id_type=pl.DeviceIdType.MESH)
 
     def give(arr, dest):
         return pltpu.make_async_remote_copy(
-            src_ref=stage_s.at[arr, dest], dst_ref=y_hbm.at[me, arr],
+            src_ref=stage_s.at[arr, dest], dst_ref=y_hbm[arr].at[me],
             send_sem=out_send.at[arr, dest], recv_sem=out_recv.at[arr, me],
             device_id={'cp': dest}, device_id_type=pl.DeviceIdType.MESH)
 
     def keep(arr, src):
-        return pltpu.make_async_copy(stage_s.at[arr, me], y_hbm.at[src, arr], out_recv.at[arr, src])
+        return pltpu.make_async_copy(stage_s.at[arr, me], y_hbm[arr].at[src], out_recv.at[arr, src])
 
     def hand_out(arr, dest):
         @pl.when(dest != me)
@@ -63,6 +68,42 @@
         @pl.when(dest == me)
         def _():
             keep(arr, me).start()
+
+    core = lax.rem(me, 2)
+    chip = me // 2
+    partner = 2 * chip + 1 - core
+    peers = [2 * lax.rem(chip + step, n_dev // 2) + core for step in range(1, n_dev // 2)]
+    cousins = [2 * lax.rem(chip + step, n_dev // 2) + 1 - core for step in range(1, n_dev // 2)]
+
+    def send_table(slot, src_ref, owner, dest):
+        return pltpu.make_async_remote_copy(
+            src_ref=src_ref, dst_ref=tab_hbm.at[owner],
+            send_sem=tab_send.at[slot], recv_sem=tab_recv.at[owner],
+            device_id={'cp': dest}, device_id_type=pl.DeviceIdType.MESH)
+
+    def table_here(owner):
+        return pltpu.make_async_copy(table_hbm, tab_hbm.at[owner], tab_recv.at[owner])
+
+    def send_dw(slot, src_ref, owner, dest):
+        return pltpu.make_async_remote_copy(
+            src_ref=src_ref, dst_ref=dw_hbm.at[owner],
+            send_sem=dw_send.at[slot], recv_sem=dw_recv.at[owner],
+            device_id={'cp': dest}, device_id_type=pl.DeviceIdType.MESH)
+
+    def dw_here(owner):
+        return pltpu.make_async_copy(dw_s, dw_hbm.at[owner], dw_recv.at[owner])
+
+    def load_table(m, slot):
+        return pltpu.make_async_copy(tab_hbm.at[m], tbuf_s.at[slot], load_sem.at[slot])
+
+    def start_load(m, slot):
+        @pl.when(m != me)
+        def _():
+            load_table(m, slot).start()
+
+        @pl.when(m == me)
+        def _():
+            pltpu.make_async_copy(table_hbm, tbuf_s.at[slot], load_sem.at[slot]).start()
 
     barrier = pltpu.get_barrier_semaphore()
     for step in range(1, n_dev):
@@ -73,6 +114,9 @@
         for step in range(1, n_dev):
             depart(arr, lax.rem(me + step, n_dev)).start()
         arrive(arr, me).start()
+    direct = peers + [partner]
+    for slot, dest in enumerate(direct):
+        send_table(slot, table_hbm, me, dest).start()
 
     sums_ref[...] = jnp.zeros_like(sums_ref)
     dk_s[...] = jnp.zeros_like(dk_s)
@@ -101,6 +145,12 @@
 
     @pl.loop(0, n_tiles)
     def _(i):
+        @pl.when(i == n_tiles - 2)
+        def _():
+            for slot, owner in enumerate(peers):
+                table_here(owner).wait()
+                send_table(len(direct) + slot, tab_hbm.at[owner], owner, partner).start()
+
         for arr in order[:3]:
             arrive(arr, i).wait()
         for b in range(nb):
@@ -173,6 +223,13 @@
         @pl.when(i > 0)
         def _():
             hand_out(1, i - 1)
+
+        @pl.when(i == n_tiles - 1)
+        def _():
+            for owner in [partner] + cousins:
+                table_here(owner).wait()
+            start_load(n_tiles - 1, 0)
+            dwT_s[...] = jnp.zeros_like(dwT_s)
 
         ds_s[1] = jnp.zeros((TILE, TILE), f32)
 
@@ -204,6 +261,16 @@
 
             @pl.when(i == n_tiles - 1)
             def _():
+                slot = lax.rem(kt, 2)
+
+                @pl.when(m > 0)
+                def _():
+                    start_load(m - 1, 1 - slot)
+
+                d_rel = (dr_s[m] * inv_sqrt).astype(bf16)
+                d_rel = [dot_nn(d_rel[:, b * BLK:(b + 1) * BLK], flip).astype(bf16) for b in range(nb)]
+                load_table(m, slot).wait()
+                dwT_s[...] += dot_nn(jnp.concatenate(d_rel, axis=1), tbuf_s[slot])
                 stage_s[2, kt] = (dk_s[kt] * inv_sqrt).T.astype(bf16)
                 stage_s[3, kt] = dv_s[kt].T.astype(bf16)
 
@@ -221,35 +288,50 @@
 
     hand_out(2, n_tiles - 1)
     hand_out(3, n_tiles - 1)
-    for t in range(n_tiles):
-        d_rel = (dr_s[t] * inv_sqrt).T.astype(bf16)
-        for b in range(nb):
-            drel_ref[pl.ds(t * TILE + b * BLK, BLK), :] = dot_nn(flip, d_rel[b * BLK:(b + 1) * BLK]).astype(bf16)
+    dw_s[0:model_dim, :] = dwT_s[...].T
+    dw_s[model_dim:, :] = sums_ref[...]
     hand_out(1, n_tiles - 1)
+    for slot, dest in enumerate(direct):
+        send_dw(slot, dw_s, me, dest).start()
+    dw_here(me).start()
     for step in range(1, n_dev):
         dest = lax.rem(me + step, n_dev)
         for arr in range(5):
             depart(arr, dest).wait_send()
         for arr in range(4):
             give(arr, dest).wait_send()
+    for slot, owner in enumerate(peers):
+        dw_here(owner).wait()
+        send_dw(len(direct) + slot, dw_hbm.at[owner], owner, partner).start()
     for src in range(n_dev):
         for arr in range(4):
             keep(arr, src).wait()
-
-
-def run_head(x, u_row, v_row):
-    n_src, n_arr, rows, dim = x.shape
+    for slot in range(2 * len(direct) - 1):
+        send_table(slot, table_hbm, me, partner).wait_send()
+        send_dw(slot, dw_s, me, partner).wait_send()
+    for owner in [me, partner] + cousins:
+        dw_here(owner).wait()
+
+
+def run_head(xs, table, u_row, v_row):
+    n_src, rows, dim = xs[0].shape
+    n_arr = len(xs)
+    model_dim = table.shape[1]
     seq = n_src * rows
     n_tiles = seq // TILE
     bf16 = jnp.bfloat16
     f32 = jnp.float32
     vmem = pl.BlockSpec(memory_space=pltpu.VMEM)
+    anywhere = pl.BlockSpec(memory_space=pl.ANY)
     tall = pltpu.VMEM((seq, dim), bf16)
     return pl.pallas_call(
         head_kernel,
-        out_shape=(jax.ShapeDtypeStruct((n_src, 4, rows, dim), bf16), jax.ShapeDtypeStruct((seq, dim), bf16), jax.ShapeDtypeStruct((8, dim), f32)),
-        in_specs=[pl.BlockSpec(memory_space=pl.ANY), vmem, vmem],
-        out_specs=(pl.BlockSpec(memory_space=pl.ANY), vmem, vmem),
+        out_shape=tuple([jax.ShapeDtypeStruct((n_src, rows, dim), bf16)] * 4) + (
+            jax.ShapeDtypeStruct((n_src, rows, model_dim), bf16),
+            jax.ShapeDtypeStruct((n_src, model_dim + 8, dim), f32),
+        ),
+        in_specs=[anywhere] * 6 + [vmem, vmem],
+        out_specs=(anywhere,) * 6,
         scratch_shapes=[
             tall, tall, tall, tall, tall,
             pltpu.VMEM((n_tiles, TILE, TILE), f32),
@@ -269,15 +351,24 @@
             pltpu.VMEM((n_tiles, dim, TILE), f32),
             pltpu.VMEM((n_tiles, dim, TILE), f32),
             pltpu.VMEM((4, n_src, rows, dim), bf16),
+            pltpu.VMEM((8, dim), f32),
+            pltpu.VMEM((2, rows, model_dim), bf16),
+            pltpu.VMEM((dim, model_dim), f32),
+            pltpu.VMEM((model_dim + 8, dim), f32),
             pltpu.SemaphoreType.DMA((n_arr, n_src)),
             pltpu.SemaphoreType.DMA((n_arr, n_src)),
             pltpu.SemaphoreType.DMA((4, n_src)),
             pltpu.SemaphoreType.DMA((4, n_src)),
+            pltpu.SemaphoreType.DMA((n_src - 1,)),
+            pltpu.SemaphoreType.DMA((n_src,)),
+            pltpu.SemaphoreType.DMA((n_src - 1,)),
+            pltpu.SemaphoreType.DMA((n_src,)),
+            pltpu.SemaphoreType.DMA((2,)),
         ],
-        compiler_params=pltpu.CompilerParams(vmem_limit_bytes=60 * 1024 * 1024, collective_id=0, has_side_effects=True),
+        compiler_params=pltpu.CompilerParams(vmem_limit_bytes=66 * 1000 * 1000, collective_id=0, has_side_effects=True),
         cost_estimate=pl.CostEstimate(flops=9 * seq * seq * dim, bytes_accessed=4 * seq * n_arr * dim, transcendentals=seq * seq // 2),
         name='rel_attention_head',
-    )(x, u_row, v_row)
+    )(*xs, table, u_row, v_row)
 
 
 def solution(mesh):
@@ -291,18 +382,14 @@
         f32 = jnp.float32
         bf16 = jnp.bfloat16
         me = lax.axis_index('cp')
-        table_all = lax.all_gather(rel_table, 'cp', axis=0, tiled=True)
         rel_mine = jnp.dot(rel_table, w_rel.reshape(model_dim, num_heads * head_dim), preferred_element_type=f32)
         rel_mine = rel_mine.astype(bf16).reshape(block_len, num_heads, head_dim)
-        packed = jnp.stack([q, k, v, d_out, rel_mine], axis=0).transpose(2, 0, 1, 3)
+        xs = [arr.transpose(1, 0, 2) for arr in (q, k, v, d_out, rel_mine)]
         u_row = lax.dynamic_slice_in_dim(u_bias, me, 1, 0)
         v_row = lax.dynamic_slice_in_dim(v_bias, me, 1, 0)
-        y, d_rel, sums = run_head(packed, u_row, v_row)
-        back = y.transpose(1, 2, 0, 3)
-        d_w = lax.dot_general(table_all, d_rel, (((0,), (0,)), ((), ())), preferred_element_type=f32)
-        tail = lax.all_gather(jnp.concatenate([d_w, sums], axis=0), 'cp')
-        d_w_rel = tail[:, :model_dim].transpose(1, 0, 2)
-        return back[0], back[1], back[2], back[3], tail[:, model_dim], tail[:, model_dim + 1], d_w_rel
+        *ys, _, tail = run_head(xs, rel_table, u_row, v_row)
+        outs = [y.transpose(1, 0, 2) for y in ys]
+        return (*outs, tail[:, model_dim], tail[:, model_dim + 1], tail[:, :model_dim].transpose(1, 0, 2))
 
     return jax.shard_map(
         local_fn,

time: 403 us -> 341 us (0.85)
  the two profiles are of different devices: /device:TPU:0 before, /device:TPU:7 now
where the time goes in v3:
time: 341 us; the launch traced here: 340 us
  Pallas kernels  309 us (91%)
  local copies, waits for them, and re-layouts  26.4 us (8%)
  matrix products  3.85 us (1%)
    pallas_call x1, Pallas kernels, run_head(): pl.pallas_call(head_kernel, out_shape=tuple([jax.ShapeDtypeStruct((n_src,...  309 us
    unnamed x17, local copies, waits for them, and re-layouts  16.1 us

profile of v3, /device:TPU:7, one launch (start us, length us, event | category | flops | bytes accessed | tf_op | source)
XLA Modules:
  0.0 340.5 jit_solution(2551998918714364296)
XLA Ops:
  0.6 1.2 constant_dynamic-slice_fusion
  1.9 3.8 %fusion.3 = bf16[768,1024]{1,0:T(8,128)(2,1)S(1)} fusion(bf16[768,1024]{1,0:T(8,128)(2,1)} %table_hbm.1, bf16[128,8,8,128]{3,2,1,0:T(8,128)(2,1)} %bitcast.33), kind=kOutput, calls=%fused_computation.4 | convolution fusion | flops 1611399168 | bytes 5242880 | tf_op jit(solution)/shard_map/dot_general | solution.py:385
  5.7 0.7 copy.28
  6.4 0.0 copy-start.3
  6.4 1.6 copy.29
  8.0 0.0 copy-done.3
  8.0 0.0 copy-start.4
  8.0 3.8 %copy_bitcast_fusion.2 = (bf16[8,768,128]{2,1,0:T(8,128)(2,1)}, bf16[8,768,128]{2,1,0:T(8,128)(2,1)}) fusion(bf16[768,8,128]{2,1,0:T(8,128)(2,1)S(1)} %copy-done.3, bf16[768,8,128]{2,1,0:T(8,128)(2,1)} %param.8), kind=kLoop, calls=%fused_computation.7 | loop fusion | bytes 6291456 | tf_op jit(solution)/shard_map/transpose | solution.py:387
  11.8 0.0 copy-done.4
  11.8 0.0 copy-done.5
  11.8 2.2 copy_bitcast_fusion
  14.0 309.5 %rel_attention_head.1 = (bf16[8,768,128]{2,1,0:T(8,128)(2,1)}, bf16[8,768,128]{2,1,0:T(8,128)(2,1)}, bf16[8,768,128]{2,1,0:T(8,128)(2,1)}, bf16[8,768,128]{2,1,0...) custom-call(bf16[8,768,128]{2,1,0:T(8,128)(2,1)} %get-tuple-element.38.xq_hbm, ...), custom_call_target="tpu_custom_call" | custom-call | flops 43486543872 | bytes 15728640 | tf_op jit(solution)/shard_map/rel_attention_head/pallas_call | solution.py:327
  323.5 0.0 copy-start
  323.5 3.7 %copy.30 = bf16[768,8,128]{2,1,0:T(8,128)(2,1)} copy(bf16[768,8,128]{2,0,1:T(8,128)(2,1)} %bitcast.30) | data formatting | bytes 3145728
  327.2 3.6 %copy.31 = bf16[768,8,128]{2,1,0:T(8,128)(2,1)} copy(bf16[768,8,128]{2,0,1:T(8,128)(2,1)} %bitcast.29) | data formatting | bytes 3145728
  330.8 0.0 copy-done
  330.8 0.6 fusion.6
  331.4 0.3 slice_bitcast_fusion
  331.7 0.0 copy-start.2
  331.7 4.4 %copy.34 = f32[1024,8,128]{2,1,0:T(8,128)} copy(f32[1024,8,128]{2,0,1:T(8,128)S(1)} %slice_bitcast_fusion) | data formatting | bytes 8388608
  336.1 0.0 copy-done.2
  336.1 2.2 copy.32
  338.3 0.0 copy-done.1
  338.3 2.2 copy.33
  (2 shorter events, 0.0 us)
Async XLA Ops:
  6.4 1.6 copy-start.3
  8.0 3.8 %copy-start.4 = (bf16[768,8,128]{2,1,0:T(8,128)(2,1)S(1)}, bf16[768,8,128]{2,1,0:T(8,128)(2,1)}, u32[]{:S(2)}) copy-start(bf16[768,8,128]{2,1,0:T(8,128)(2,1)} %param.15) | copy-start | bytes 4718596
  8.0 3.8 %copy-start.5 = (bf16[768,8,128]{2,1,0:T(8,128)(2,1)S(1)}, bf16[768,8,128]{2,1,0:T(8,128)(2,1)}, u32[]{:S(2)}) copy-start(bf16[768,8,128]{2,1,0:T(8,128)(2,1)} %param.10) | copy-start | bytes 4718596
  323.5 7.3 %copy-start = (f32[8,1032,128]{2,1,0:T(8,128)S(1)}, f32[8,1032,128]{2,1,0:T(8,128)}, u32[]{:S(2)}) copy-start(f32[8,1032,128]{2,1,0:T(8,128)} %get-tuple-element.16) | copy-start | bytes 12681220
  331.7 4.5 %copy-start.2 = (bf16[8,768,128]{2,1,0:T(8,128)(2,1)S(1)}, bf16[8,768,128]{2,1,0:T(8,128)(2,1)}, u32[]{:S(2)}) copy-start(bf16[8,768,128]{2,1,0:T(8,128)(2,1)} %get-tuple-element.14) | copy-start | bytes 4718596
  336.1 2.2 copy-start.1
